TPU v7x, 32 devices: a whole 2x2x4 slice. The times are simulated.
32 devices in a mesh: seq: 8 (over y, x, core), rep: 4 (over z).
Axes of the slice: x: 2, y: 2, z: 4, core: 2. Of those that a mesh axis runs over, the one named last changes fastest.
Arguments:
- queries: bfloat16 [4096, 2048], P(('rep', 'seq')), parts along dimension 0, may hold values from -6 to 6
- keys: bfloat16 [4096, 2048], P(('rep', 'seq')), parts along dimension 0, may hold values from -6 to 6
- values: bfloat16 [4096, 2048], P(('rep', 'seq')), parts along dimension 0, may hold values from -6 to 6
- short_taps: float32 [3, 3, 2048], replicated, may hold values from -3.5 to 3.5
- decay: float32 [2048, 16], replicated, may hold values from 0.00048828125 to 0.1
- residue: float32 [2048, 16], replicated, may hold values from -1.5 to 1.5
- skip: float32 [2048], replicated, may hold values from -3 to 3
- w_out: bfloat16 [2048, 2048], replicated, may hold values from -0.125 to 0.125
Outputs:
- layer_out: bfloat16 [4096, 2048], P(('rep', 'seq')), parts along dimension 0
There are 4 independent parts, one for each index of `rep`. A program takes and returns all parts, laid end to end along the dimension named above; an argument that names none is the same for every part. Nothing has to cross between parts.
All inputs are finite; a program needn't handle non-finite values.
Results may differ from a plain program's by a relative error of at most 0.014.
Values may be sent and summed in bfloat16 or wider, within the bound.
A program may use at most 64 MiB of HBM per device.

v0:
```python
import functools
import math

import jax
import jax.numpy as jnp
from jax import lax
from jax.experimental import pallas as pl
from jax.experimental.pallas import tpu as pltpu
from jax.sharding import PartitionSpec as P

MESH = pl.DeviceIdType.MESH
F32 = jnp.float32
SUB = 8


def kernel(
    n, width,
    q_hbm, k_hbm, v_hbm, taps_hbm, rates_hbm, residue_hbm, skip_hbm, w_hbm,
    out_ref,
    q_in, k_in, v_in, taps_ref, rates_ref, residue_ref, skip_ref, w_in, tails_out, tails_in, ext, sig, q_short, partial, states,
    carry_table, tap_table, gated, ends, before, totals, earlier, total_out,
    in_sems, w_sem, tail_sems, pair_send, pair_recv, group_send, group_recv,
):
    rows, chans = q_in.shape
    modes = rates_ref.shape[0]
    blocks = rows // SUB
    chunks = chans // width
    groups = n // 2
    me = lax.axis_index("seq")
    group = lax.div(me, 2)
    odd = lax.rem(me, 2)

    barrier = pltpu.get_barrier_semaphore()

    def greet(step, carry):
        pl.semaphore_signal(
            barrier, inc=1, device_id={"seq": lax.rem(me + step, n)}, device_id_type=MESH
        )
        return carry

    lax.fori_loop(1, n, greet, 0)
    loads = [
        pltpu.make_async_copy(src, dst, in_sems.at[i])
        for i, (src, dst) in enumerate((
            (q_hbm, q_in), (k_hbm, k_in), (v_hbm, v_in), (rates_hbm, rates_ref),
            (residue_hbm, residue_ref), (skip_hbm, skip_ref), (taps_hbm, taps_ref),
        ))
    ]
    for load in loads:
        load.start()
    w_load = pltpu.make_async_copy(w_hbm, w_in, w_sem)
    w_load.start()

    for load in loads[:3]:
        load.wait()
    for i, tokens in enumerate((q_in, k_in, v_in)):
        last = tokens[rows - 16 :, :].astype(F32)
        tails_out[2 * i : 2 * i + 2, :] = last[14:16]
    tails_out[6:8, :] = jnp.zeros((2, chans), F32)
    pl.semaphore_wait(barrier, n - 1)

    def tail_copy():
        return pltpu.make_async_remote_copy(
            src_ref=tails_out, dst_ref=tails_in, send_sem=tail_sems.at[0], recv_sem=tail_sems.at[1],
            device_id={"seq": lax.rem(me + 1, n)}, device_id_type=MESH,
        )

    def pair_copy(g):
        return pltpu.make_async_remote_copy(
            src_ref=ends.at[g], dst_ref=before.at[g], send_sem=pair_send.at[g], recv_sem=pair_recv.at[g],
            device_id={"seq": me + 1 - 2 * odd}, device_id_type=MESH,
        )

    def group_copy(source, target, core, g):
        return pltpu.make_async_remote_copy(
            src_ref=totals.at[g], dst_ref=earlier.at[source, g],
            send_sem=group_send.at[target, core, g], recv_sem=group_recv.at[source, g],
            device_id={"seq": 2 * target + core}, device_id_type=MESH,
        )

    @pl.when(me < n - 1)
    def _():
        tail_copy().start()

    @pl.when(me == 0)
    def _():
        tails_in[...] = jnp.zeros_like(tails_in)

    @pl.when(odd == 0)
    def _():
        before[...] = jnp.zeros_like(before)

    for load in loads[3:]:
        load.wait()

    place = lax.broadcasted_iota(jnp.int32, (SUB, width), 0)
    steps = (place + 1).astype(F32)

    def tables(g, carry):
        cols = pl.ds(pl.multiple_of(g * width, width), width)
        rates = rates_ref[:, cols]
        weights = residue_ref[:, cols] * jnp.sqrt(1.0 - jnp.exp(-2.0 * rates))
        total = jnp.zeros((SUB, width), F32)
        for m in range(modes):
            row = jnp.exp(-rates[m : m + 1] * steps) * weights[m : m + 1]
            carry_table[m * SUB : (m + 1) * SUB, cols] = row
            total = total + row
        first = jnp.sum(weights, axis=0, keepdims=True) + skip_ref[:, cols]
        taps = jnp.where(place == 0, first, pltpu.roll(total, 1, 0))
        for s in range(SUB):
            shifted = taps if s == 0 else jnp.where(place >= s, pltpu.roll(taps, s, 0), 0.0)
            tap_table[s * SUB : (s + 1) * SUB, cols] = shifted
        return carry

    lax.fori_loop(0, chunks, tables, 0)

    strip = math.gcd(rows, 16)

    def mix(g, first, last):
        cols = pl.ds(pl.multiple_of(g * width, width), width)
        for i, tokens in enumerate((q_in, k_in, v_in)):
            for r in range(max(first - strip, 0), last, strip):
                ext[i, SUB + r : SUB + r + strip, :] = tokens[r : r + strip, cols].astype(F32)

        def short(i, r):
            result = taps_ref[i, 0:1, cols] * ext[i, SUB + r : SUB + r + strip, :]
            result = result + taps_ref[i, 1:2, cols] * ext[i, SUB + r - 1 : SUB + r + strip - 1, :]
            return result + taps_ref[i, 2:3, cols] * ext[i, SUB + r - 2 : SUB + r + strip - 2, :]

        for r in range(first, last, strip):
            mixed = (short(1, r) * short(2, r)).astype(jnp.bfloat16)
            mixed = mixed.astype(F32)
            for j in range(0, strip, SUB):
                sig[(r + j) // SUB, :, cols] = mixed[j : j + SUB]
            q_short[r : r + strip, cols] = short(0, r)

    def mix_later(g, carry):
        mix(g, strip, rows)
        return carry

    lax.fori_loop(0, chunks, mix_later, 0)

    @pl.when(me > 0)
    def _():
        tail_copy().wait_recv()

    def combine(g):
        @pl.when(odd == 1)
        def _():
            pair_copy(g).wait_recv()

            @pl.when(group < groups - 1)
            def _():
                cols = pl.ds(pl.multiple_of(g * width, width), width)
                span = jnp.exp(-float(rows) * rates_ref[:, cols])
                totals[g] = (span * before[g] + ends[g]).astype(totals.dtype)

                def send(target, carry):
                    for core in range(2):
                        group_copy(group, target, core, g).start()
                    return carry

                lax.fori_loop(group + 1, groups, send, 0)

    def local(g, carry):
        cols = pl.ds(pl.multiple_of(g * width, width), width)
        for i in range(3):
            ext[i, SUB - 2 : SUB, :] = tails_in[2 * i : 2 * i + 2, cols]
        mix(g, 0, strip)
        fade = jnp.exp(-rates_ref[:, cols])

        def block(b, state):
            states[b, :, cols] = state
            base = pl.multiple_of(b * SUB, SUB)
            acc = None
            for s in range(SUB):
                row = sig[b, s : s + 1, cols]
                state = state * fade + row
                term = tap_table[s * SUB : (s + 1) * SUB, cols] * row
                acc = term if acc is None else acc + term
            partial[pl.ds(base, SUB), cols] = acc
            return state

        ends[g] = lax.fori_loop(0, blocks, block, jnp.zeros((modes, width), F32), unroll=2)

        @pl.when(odd == 0)
        def _():
            pair_copy(g).start()

        @pl.when(g > 0)
        def _():
            combine(g - 1)

        return carry

    lax.fori_loop(0, chunks, local, 0)
    combine(chunks - 1)
    w_load.wait()
    batch = 4 if blocks % 4 == 0 else 1
    tile = out_ref.shape[1] // (blocks // batch)

    def project(g, side, k):
        source = pl.ds(pl.multiple_of(g * width, width), width)
        here = pl.ds(pl.multiple_of(k * tile, tile), tile)
        piece = jnp.dot(gated[side], w_in[source, here], preferred_element_type=F32)
        total_out[:, here] += piece

    def finish(g, carry):
        cols = pl.ds(pl.multiple_of(g * width, width), width)
        rates = rates_ref[:, cols]
        far = jnp.exp(-2.0 * rows * rates)

        def gather(source, state):
            group_copy(source, group, odd, g).wait_recv()
            return state * far + earlier[source, g].astype(F32)

        entering = lax.fori_loop(0, group, gather, jnp.zeros((modes, width), F32))
        span = jnp.where(odd == 1, jnp.exp(-float(rows) * rates), 1.0)
        entering = span * entering + before[g]
        fade = jnp.exp(-float(SUB) * rates)
        for b in range(blocks):
            states[b, :, cols] = states[b, :, cols] + entering
            entering = entering * fade

        side = lax.rem(g, 2)

        def outputs(k, inner):
            project(jnp.maximum(g - 1, 0), 1 - side, k)
            base = pl.multiple_of(k * batch * SUB, batch * SUB)
            accs = [partial[pl.ds(base + j * SUB, SUB), cols] for j in range(batch)]
            for m in range(modes):
                table = carry_table[m * SUB : (m + 1) * SUB, cols]
                for j in range(batch):
                    row = states[k * batch + j, m : m + 1, cols]
                    accs[j] = accs[j] + table * row
            long_out = jnp.concatenate(accs, axis=0).astype(jnp.bfloat16).astype(F32)
            here = pl.ds(base, batch * SUB)
            gated[side, here, :] = (q_short[here, cols] * long_out).astype(jnp.bfloat16)
            return inner

        lax.fori_loop(0, blocks // batch, outputs, 0)
        return carry

    gated[1] = jnp.zeros(gated.shape[1:], gated.dtype)
    total_out[...] = jnp.zeros_like(total_out)
    lax.fori_loop(0, chunks, finish, 0)
    for k in range(blocks // batch):
        here = slice(k * tile, (k + 1) * tile)
        piece = jnp.dot(
            gated[(chunks - 1) % 2], w_in[chans - width :, here], preferred_element_type=F32
        )
        out_ref[:, here] = (total_out[:, here] + piece).astype(out_ref.dtype)

    @pl.when(me < n - 1)
    def _():
        tail_copy().wait_send()

    @pl.when(odd == 0)
    def _():
        for g in range(chunks):
            pair_copy(g).wait_send()

    @pl.when(odd == 1)
    def _():
        def sent(target, carry):
            for core in range(2):
                for g in range(chunks):
                    group_copy(group, target, core, g).wait_send()
            return carry

        lax.fori_loop(group + 1, groups, sent, 0)


def solution(mesh):
    n = mesh.shape["seq"]

    def body(queries, keys, values, short_taps, decay, residue, skip, w_out):
        rows, chans = queries.shape
        modes = decay.shape[1]
        width = math.gcd(chans, 512)
        chunks = chans // width
        bf16 = jnp.bfloat16
        vmem = pl.BlockSpec(memory_space=pltpu.VMEM)
        hbm = pl.BlockSpec(memory_space=pl.ANY)
        dma = pltpu.SemaphoreType.DMA
        return pl.pallas_call(
            functools.partial(kernel, n, width),
            out_shape=jax.ShapeDtypeStruct((rows, w_out.shape[1]), bf16),
            in_specs=[hbm] * 8,
            out_specs=vmem,
            scratch_shapes=[
                pltpu.VMEM((rows, chans), bf16),
                pltpu.VMEM((rows, chans), bf16),
                pltpu.VMEM((rows, chans), bf16),
                pltpu.VMEM(short_taps.shape, F32),
                pltpu.VMEM((modes, chans), F32),
                pltpu.VMEM((modes, chans), F32),
                pltpu.VMEM((1, chans), F32),
                pltpu.VMEM(w_out.shape, bf16),
                pltpu.VMEM((SUB, chans), F32),
                pltpu.VMEM((SUB, chans), F32),
                pltpu.VMEM((3, rows + SUB, width), F32),
                pltpu.VMEM((rows // SUB, SUB, chans), F32),
                pltpu.VMEM((rows, chans), F32),
                pltpu.VMEM((rows, chans), F32),
                pltpu.VMEM((rows // SUB, modes, chans), F32),
                pltpu.VMEM((modes * SUB, chans), F32),
                pltpu.VMEM((SUB * SUB, chans), F32),
                pltpu.VMEM((2, rows, width), bf16),
                pltpu.VMEM((chunks, modes, width), F32),
                pltpu.VMEM((chunks, modes, width), F32),
                pltpu.VMEM((chunks, modes, width), bf16),
                pltpu.VMEM((n // 2, chunks, modes, width), bf16),
                pltpu.VMEM((rows, w_out.shape[1]), F32),
                dma((7,)),
                dma,
                dma((2,)),
                dma((chunks,)),
                dma((chunks,)),
                dma((n // 2, 2, chunks)),
                dma((n // 2, chunks)),
            ],
            compiler_params=pltpu.CompilerParams(
                collective_id=0, has_side_effects=True, vmem_limit_bytes=60 * 1024 * 1024
            ),
        )(queries, keys, values, short_taps, decay.T, residue.T, skip[None, :], w_out)

    placed = (P(("rep", "seq"), None),) * 3 + (P(),) * 5
    return jax.shard_map(
        body, mesh=mesh, in_specs=placed, out_specs=P(("rep", "seq"), None), check_vma=False
    )
```

profile of v0, /device:TPU:29, one launch (start us, length us, event | category | flops | bytes accessed | tf_op | source)
XLA Modules:
  0.0 18.0 jit_solution(4916957943317658486)
XLA Ops:
  0.0 16.1 %shard_map.82 = bf16[128,2048]{1,0:T(8,128)(2,1)} custom-call(bf16[128,2048]{1,0:T(8,128)(2,1)} %q_hbm.1, bf16[128,2048]{1,0:T(8,128)(2,1)} %k_hbm.1, bf16[128,2048]{1,0:T(8,128)(2,1)} %v_hbm.1, f32[3,3,2048]{2,1,0:T(4,128)} %taps_hbm.1, f32[16,2048]{1,0:T(8,128)} %bitcast.3, f32[16,2048]{1,0:T(8,128)} %bitcast.4, f32[1,2048]{1,0:T(1,128)} %bitcast.5, ...), custom_call_target="tpu_custom_call" | custom-call | tf_op jit(solution)/shard_map/pallas_call | solution.py:286
  16.1 1.9 %copy.10 = bf16[128,2048]{1,0:T(8,128)(2,1)} copy(bf16[128,2048]{1,0:T(8,128)(2,1)} %shard_map.82) | data formatting | bytes 1048576
where the time goes:
time: 18.1 us; the launch traced here: 18 us
  Pallas kernels  16.1 us (89%)
  local copies, waits for them, and re-layouts  1.88 us (10%)
    pallas_call x1, Pallas kernels, body(): pl.pallas_call(functools.partial(kernel, n, width), out_shape=jax.ShapeDt...  16.1 us
    unnamed x1, local copies, waits for them, and re-layouts  1.88 us

commit v1 on v0

--- a/solution.py
+++ b/solution.py
@@ -285,7 +285,7 @@
         dma = pltpu.SemaphoreType.DMA
         return pl.pallas_call(
             functools.partial(kernel, n, width),
-            out_shape=jax.ShapeDtypeStruct((rows, w_out.shape[1]), bf16),
+            out_shape=pltpu.VMEM((rows, w_out.shape[1]), bf16),
             in_specs=[hbm] * 8,
             out_specs=vmem,
             scratch_shapes=[
@@ -321,9 +321,9 @@
                 dma((n // 2, chunks)),
             ],
             compiler_params=pltpu.CompilerParams(
-                collective_id=0, has_side_effects=True, vmem_limit_bytes=60 * 1024 * 1024
+                collective_id=0, has_side_effects=True, vmem_limit_bytes=40 * 1024 * 1024
             ),
-        )(queries, keys, values, short_taps, decay.T, residue.T, skip[None, :], w_out)
+        )(*(pltpu.with_memory_space_constraint(x, pltpu.HBM) for x in (queries, keys, values, short_taps, decay.T, residue.T, skip[None, :], w_out)))
 
     placed = (P(("rep", "seq"), None),) * 3 + (P(),) * 5
     return jax.shard_map(

time: 18.1 us -> 16.3 us (0.901)
  local copies, waits for them, and re-layouts: 1.88 us -> 0.8 us
  Pallas kernels: 16.1 us -> 15.3 us
    unnamed x1, local copies, waits for them, and re-layouts: 1.88 us -> 0.8 us
    pallas_call x1, Pallas kernels: 16.1 us -> 15.3 us  [body(): pl.pallas_call(functools.partial(kernel, n, width), out_shape=pltpu.VMEM(...]
where the time goes in v1:
time: 16.3 us; the launch traced here: 16.1 us
  Pallas kernels  15.3 us (94%)
  local copies, waits for them, and re-layouts  0.8 us (5%)
    pallas_call x1, Pallas kernels, body(): pl.pallas_call(functools.partial(kernel, n, width), out_shape=pltpu.VMEM(...  15.3 us
    unnamed x1, local copies, waits for them, and re-layouts  0.8 us

profile of v1, /device:TPU:29, one launch (start us, length us, event | category | flops | bytes accessed | tf_op | source)
XLA Modules:
  0.0 16.1 jit_solution(6196596114427820745)
XLA Ops:
  0.0 15.3 %shard_map.82 = bf16[128,2048]{1,0:T(8,128)(2,1)S(1)} custom-call(bf16[128,2048]{1,0:T(8,128)(2,1)} %q_hbm.1, bf16[128,2048]{1,0:T(8,128)(2,1)} %k_hbm.1, bf16[128,2048]{1,0:T(8,128)(2,1)} %v_hbm.1, f32[3,3,2048]{2,1,0:T(4,128)} %taps_hbm.1, f32[16,2048]{1,0:T(8,128)} %bitcast.3, f32[16,2048]{1,0:T(8,128)} %bitcast.4, f32[1,2048]{1,0:T(1,128)} %bitcast.5, ...), custom_call_target="tpu_custom_call" | custom-call | tf_op jit(solution)/shard_map/pallas_call | solution.py:286
  15.3 0.8 %copy.10 = bf16[128,2048]{1,0:T(8,128)(2,1)} copy(bf16[128,2048]{1,0:T(8,128)(2,1)S(1)} %shard_map.82) | data formatting | bytes 1048576

commit v2 on v1

v2 whole, which is shorter than its diff:
```python
import functools
import math

import jax
import jax.numpy as jnp
from jax import lax
from jax.experimental import pallas as pl
from jax.experimental.pallas import tpu as pltpu
from jax.sharding import PartitionSpec as P

MESH = pl.DeviceIdType.MESH
F32 = jnp.float32
BF16 = jnp.bfloat16
SUB = 8
LANES = 128


def kernel(
    n, width,
    q_hbm, k_hbm, v_hbm, taps_hbm, rates_hbm, residue_hbm, skip_hbm, w_hbm,
    out_ref,
    q_in, k_in, v_in, taps_ref, rates_ref, residue_ref, skip_ref, w_in,
    tails_out, tails_in, order, moved, fade_ref, skip2_ref, stride_ref, span_ref, weight_ref,
    filter_ref, edge, sig, q_short, partial, local, segments, turn, natural,
    gated, entry, ends, before, totals, earlier, total_out,
    in_sems, w_sem, tail_sems, pair_send, pair_recv, group_send, group_recv, credits,
):
    rows, chans = q_in.shape
    modes = rates_ref.shape[0]
    steps = rows // SUB
    chunks = chans // width
    cells = width // LANES
    groups = n // 2
    me = lax.axis_index("seq")
    group = lax.div(me, 2)
    odd = lax.rem(me, 2)

    barrier = pltpu.get_barrier_semaphore()

    def greet(device):
        pl.semaphore_signal(barrier, inc=1, device_id={"seq": device}, device_id_type=MESH)

    @pl.when(me > 0)
    def _():
        greet(me - 1)

    @pl.when(odd == 1)
    def _():
        def later(device, carry):
            greet(device)
            return carry

        lax.fori_loop(me + 1, n, later, 0)

    loads = [
        pltpu.make_async_copy(src, dst, in_sems.at[i])
        for i, (src, dst) in enumerate((
            (rates_hbm, rates_ref), (k_hbm, k_in), (v_hbm, v_in), (taps_hbm, taps_ref),
            (residue_hbm, residue_ref), (q_hbm, q_in), (skip_hbm, skip_ref),
        ))
    ]
    for load in loads:
        load.start()
    w_load = pltpu.make_async_copy(w_hbm, w_in, w_sem)
    w_load.start()

    def tail_copy():
        return pltpu.make_async_remote_copy(
            src_ref=tails_out, dst_ref=tails_in, send_sem=tail_sems.at[0], recv_sem=tail_sems.at[1],
            device_id={"seq": lax.rem(me + 1, n)}, device_id_type=MESH,
        )

    def pair_copy(g):
        return pltpu.make_async_remote_copy(
            src_ref=ends.at[g], dst_ref=before.at[g], send_sem=pair_send.at[g], recv_sem=pair_recv.at[g],
            device_id={"seq": me + 1 - 2 * odd}, device_id_type=MESH,
        )

    def group_copy(source, target, core, g):
        return pltpu.make_async_remote_copy(
            src_ref=totals.at[g], dst_ref=earlier.at[source, g],
            send_sem=group_send.at[target, core, g], recv_sem=group_recv.at[source, g],
            device_id={"seq": 2 * target + core}, device_id_type=MESH,
        )

    place = lax.broadcasted_iota(jnp.int32, order.shape, 0)
    token = lax.broadcasted_iota(jnp.int32, order.shape, 1)
    wanted = steps * lax.rem(place, SUB) + lax.div(place, SUB) - 2
    order[...] = jnp.where(token == wanted, 1.0, 0.0).astype(BF16)

    @pl.when(me == 0)
    def _():
        tails_in[...] = jnp.zeros_like(tails_in)

    @pl.when(odd == 0)
    def _():
        before[...] = jnp.zeros_like(before)

    total_out[...] = jnp.zeros_like(total_out)
    natural[...] = jnp.zeros_like(natural)
    lane_row = lax.broadcasted_iota(jnp.int32, (SUB, LANES), 0)
    lane_step = lane_row.astype(F32)

    def columns(c):
        return pl.ds(pl.multiple_of(c * LANES, LANES), LANES)

    def chunk(g):
        return pl.ds(pl.multiple_of(g * width, width), width)

    loads[0].wait()

    def rates_tables(g, carry):
        cols = chunk(g)
        rates = rates_ref[:, cols]
        fade_ref[:, cols] = jnp.exp(-rates)
        skip2_ref[:, cols] = jnp.exp(-float(steps - 2) * rates)
        stride_ref[:, cols] = jnp.exp(-float(steps) * rates)
        span_ref[:, cols] = jnp.exp(-float(rows) * rates)
        return carry

    lax.fori_loop(0, chunks, rates_tables, 0)

    for load in loads[1:4]:
        load.wait()

    def short(x, taps, i):
        result = taps[0] * x[SUB * (i + 2) : SUB * (i + 3)]
        result = result + taps[1] * x[SUB * (i + 1) : SUB * (i + 2)]
        return result + taps[2] * x[SUB * i : SUB * (i + 1)]

    def tap_rows(which, cols):
        return [taps_ref[which, j : j + 1, cols] for j in range(3)]

    wide = min(2, cells) * LANES
    strips = chans // wide

    def strip(c):
        return pl.ds(pl.multiple_of(c * wide, wide), wide)

    def arrange(tokens, c):
        return jnp.dot(order[...], tokens[:, strip(c)], preferred_element_type=F32)

    def rounded(x):
        return x.astype(BF16).astype(F32)

    def mix(c, carry):
        slot = lax.rem(c, 2)
        following = jnp.minimum(c + 1, strips - 1)
        next_k = arrange(k_in, following)
        next_v = arrange(v_in, following)
        for half in range(wide // LANES):
            cols = columns(c * (wide // LANES) + half)
            xk = moved.at[slot, 0, :, half * LANES : (half + 1) * LANES]
            xv = moved.at[slot, 1, :, half * LANES : (half + 1) * LANES]
            k_taps = tap_rows(1, cols)
            v_taps = tap_rows(2, cols)
            for i in range(2):
                edge[i, :, cols] = short(xk, k_taps, i)
                edge[2 + i, :, cols] = short(xv, v_taps, i)
            fades = [fade_ref[m : m + 1, cols] for m in range(modes)]
            state = [None] * modes
            for i in range(2, steps):
                u = rounded(short(xk, k_taps, i) * short(xv, v_taps, i))
                sig[i, :, cols] = u
                for m in range(modes):
                    state[m] = u if i == 2 else state[m] * fades[m] + u
            for m in range(modes):
                local[m * SUB : (m + 1) * SUB, cols] = state[m]
        moved[1 - slot, 0] = next_k
        moved[1 - slot, 1] = next_v
        return carry

    moved[0, 0] = arrange(k_in, 0)
    moved[0, 1] = arrange(v_in, 0)
    first_cells = strips // 3
    lax.fori_loop(0, first_cells, mix, 0)

    loads[5].wait()
    for i, tokens in enumerate((q_in, k_in, v_in)):
        last = tokens[rows - 16 :, :].astype(F32)
        tails_out[2 * i : 2 * i + 2, :] = last[14:16]
    tails_out[6:8, :] = jnp.zeros((2, chans), F32)

    pl.semaphore_wait(barrier, jnp.where(me < n - 1, 1, 0) + group)

    @pl.when(me < n - 1)
    def _():
        tail_copy().start()

    def credit(source, carry):
        pl.semaphore_signal(
            credits.at[group], inc=1, device_id={"seq": 2 * source + 1}, device_id_type=MESH
        )
        return carry

    lax.fori_loop(0, group, credit, 0)

    lax.fori_loop(first_cells, strips, mix, 0)

    loads[4].wait()
    loads[6].wait()

    def residue_tables(g, carry):
        cols = chunk(g)
        weight_ref[:, cols] = residue_ref[:, cols] * jnp.sqrt(1.0 - jnp.exp(-2.0 * rates_ref[:, cols]))
        return carry

    lax.fori_loop(0, chunks, residue_tables, 0)

    @pl.when(me > 0)
    def _():
        tail_copy().wait_recv()

    head = lane_row == 0

    def ends_of(which, cols, zeroth, first):
        taps = tap_rows(which, cols)
        one, two = (
            jnp.where(head, tails_in[2 * which + a : 2 * which + a + 1, cols], 0.0) for a in (1, 0)
        )
        return zeroth + taps[1] * one + taps[2] * two, first + taps[2] * one

    def summarize(c, g, half):
        cols = columns(c)
        k0, k1 = ends_of(1, cols, edge[0, :, cols], edge[1, :, cols])
        v0, v1 = ends_of(2, cols, edge[2, :, cols], edge[3, :, cols])
        u0 = rounded(k0 * v0)
        u1 = rounded(k1 * v1)
        sig[0, :, cols] = u0
        sig[1, :, cols] = u1
        for m in range(modes):
            row = slice(m, m + 1)
            start = fade_ref[row, cols] * u0 + u1
            turn[half, m * SUB : (m + 1) * SUB, :] = (
                local[m * SUB : (m + 1) * SUB, cols] + skip2_ref[row, cols] * start
            )
        scale = weight_ref[:, cols] * fade_ref[:, cols]
        stride = stride_ref[:, cols]
        state = None
        for j in range(SUB):
            part = scale * turn[half, pl.ds(j, modes, stride=SUB), :]
            segments[j, :, cols] = part
            state = part if j == 0 else state * stride + part
        ends[g, :, columns(c - g * cells)] = state

    def summaries(g, carry):
        for c in range(cells):
            summarize(g * cells + c, g, c)

        @pl.when(odd == 0)
        def _():
            pair_copy(g).start()

        return carry

    lax.fori_loop(0, chunks, summaries, 0)

    def direct(c, carry):
        slot = lax.rem(c, 2)
        next_q = arrange(q_in, jnp.minimum(c + 1, strips - 1))
        for half in range(wide // LANES):
            cols = columns(c * (wide // LANES) + half)
            response = [jnp.zeros((SUB, LANES), F32) for _ in range(steps // SUB)]
            for m in range(modes):
                row = slice(m, m + 1)
                rates = rates_ref[row, cols]
                term = jnp.exp(-rates * lane_step) * weight_ref[row, cols]
                for b in range(steps // SUB):
                    response[b] = response[b] + term
                    if b + 1 < steps // SUB:
                        term = term * jnp.exp(-float(SUB) * rates)
            response[0] = response[0] + jnp.where(lane_row == 0, skip_ref[:, cols], 0.0)
            for b in range(steps // SUB):
                filter_ref[half, b * SUB : (b + 1) * SUB, :] = response[b]
            xq = moved.at[slot, 0, :, half * LANES : (half + 1) * LANES]
            q_taps = tap_rows(0, cols)
            q0, q1 = ends_of(0, cols, short(xq, q_taps, 0), short(xq, q_taps, 1))
            taps = [filter_ref[half, i : i + 1, :] for i in range(steps)]
            signal = [sig[i, :, cols] for i in range(steps)]
            for i in range(steps):
                q_short[i, :, cols] = q0 if i == 0 else q1 if i == 1 else short(xq, q_taps, i)
                acc = taps[0] * signal[i]
                for s in range(i):
                    acc = acc + taps[i - s] * signal[s]
                partial[i, :, cols] = acc
        moved[1 - slot, 0] = next_q
        return carry

    moved[0, 0] = arrange(q_in, 0)
    lax.fori_loop(0, strips, direct, 0)

    @pl.when(odd == 1)
    def _():
        def combine(g, carry):
            pair_copy(g).wait_recv()

            @pl.when(group < groups - 1)
            def _():
                totals[g] = (span_ref[:, chunk(g)] * before[g] + ends[g]).astype(totals.dtype)

                def send(target, inner):
                    @pl.when(g == 0)
                    def _():
                        pl.semaphore_wait(credits.at[target], 2)

                    for core in range(2):
                        group_copy(group, target, core, g).start()
                    return inner

                lax.fori_loop(group + 1, groups, send, 0)

            return carry

        lax.fori_loop(0, chunks, combine, 0)

    w_load.wait()
    tile = out_ref.shape[1] // cells

    def gather_gated():
        for k in range(cells):
            gated[:, k * LANES : (k + 1) * LANES] = natural[k].astype(BF16)

    def project(g, k):
        here = slice(k * tile, (k + 1) * tile)
        return jnp.dot(gated[...], w_in[chunk(g), here], preferred_element_type=F32)

    def output(g, k):
        cols = columns(g * cells + k)
        state = entry[:, k * LANES : (k + 1) * LANES]
        stride = stride_ref[:, cols]
        for j in range(SUB):
            turn[k, j * modes : (j + 1) * modes, :] = state
            if j + 1 < SUB:
                state = state * stride + segments[j, :, cols]
        flow = [turn[k, pl.ds(m, SUB, stride=modes), :] for m in range(modes)]
        for i in range(steps):
            terms = list(flow)
            while len(terms) > 1:
                terms = [sum(terms[a : a + 2]) for a in range(0, len(terms), 2)]
            long_out = rounded(partial[i, :, cols] + terms[0])
            natural[k, pl.ds(i, SUB, stride=steps), :] = q_short[i, :, cols] * long_out
            if i + 1 < steps:
                flow = [flow[m] * fade_ref[m : m + 1, cols] for m in range(modes)]

    def finish(g, carry):
        span = span_ref[:, chunk(g)]
        far = span * span

        def gather(source, state):
            group_copy(source, group, odd, g).wait_recv()
            return state * far + earlier[source, g].astype(F32)

        entering = lax.fori_loop(0, group, gather, jnp.zeros((modes, width), F32))
        entry[...] = jnp.where(odd == 1, span, 1.0) * entering + before[g]
        gather_gated()
        for k in range(cells):
            total_out[:, k * tile : (k + 1) * tile] += project(jnp.maximum(g - 1, 0), k)
            output(g, k)
        return carry

    lax.fori_loop(0, chunks, finish, 0)
    gather_gated()
    for k in range(cells):
        here = slice(k * tile, (k + 1) * tile)
        out_ref[:, here] = (total_out[:, here] + project(chunks - 1, k)).astype(out_ref.dtype)

    @pl.when(me < n - 1)
    def _():
        tail_copy().wait_send()

    @pl.when(odd == 0)
    def _():
        for g in range(chunks):
            pair_copy(g).wait_send()

    @pl.when(odd == 1)
    def _():
        def sent(target, carry):
            for core in range(2):
                for g in range(chunks):
                    group_copy(group, target, core, g).wait_send()
            return carry

        lax.fori_loop(group + 1, groups, sent, 0)


def solution(mesh):
    n = mesh.shape["seq"]

    def body(queries, keys, values, short_taps, decay, residue, skip, w_out):
        rows, chans = queries.shape
        modes = decay.shape[1]
        width = math.gcd(chans, 512)
        chunks = chans // width
        steps = rows // SUB
        hbm = pl.BlockSpec(memory_space=pl.ANY)
        dma = pltpu.SemaphoreType.DMA
        table = pltpu.VMEM((modes, chans), F32)
        tokens = pltpu.VMEM((rows, chans), BF16)
        placed = pltpu.VMEM((steps, SUB, chans), F32)
        operands = (queries, keys, values, short_taps, decay.T, residue.T, skip[None, :], w_out)
        return pl.pallas_call(
            functools.partial(kernel, n, width),
            out_shape=pltpu.VMEM((rows, w_out.shape[1]), BF16),
            in_specs=[hbm] * 8,
            out_specs=pl.BlockSpec(memory_space=pltpu.VMEM),
            scratch_shapes=[
                tokens, tokens, tokens,
                pltpu.VMEM(short_taps.shape, F32),
                table, table,
                pltpu.VMEM((1, chans), F32),
                pltpu.VMEM(w_out.shape, BF16),
                pltpu.VMEM((SUB, chans), F32),
                pltpu.VMEM((SUB, chans), F32),
                pltpu.VMEM(((steps + 2) * SUB, rows), BF16),
                pltpu.VMEM((2, 2, (steps + 2) * SUB, min(width, 2 * LANES)), F32),
                table, table, table, table, table,
                pltpu.VMEM((2, steps, LANES), F32),
                pltpu.VMEM((4, SUB, chans), F32),
                placed, placed, placed,
                pltpu.VMEM((modes * SUB, chans), F32),
                pltpu.VMEM((SUB, modes, chans), F32),
                pltpu.VMEM((width // LANES, modes * SUB, LANES), F32),
                pltpu.VMEM((width // LANES, rows, LANES), F32),
                pltpu.VMEM((rows, width), BF16),
                pltpu.VMEM((modes, width), F32),
                pltpu.VMEM((chunks, modes, width), F32),
                pltpu.VMEM((chunks, modes, width), F32),
                pltpu.VMEM((chunks, modes, width), BF16),
                pltpu.VMEM((n // 2, chunks, modes, width), BF16),
                pltpu.VMEM((rows, w_out.shape[1]), F32),
                dma((7,)),
                dma,
                dma((2,)),
                dma((chunks,)),
                dma((chunks,)),
                dma((n // 2, 2, chunks)),
                dma((n // 2, chunks)),
                pltpu.SemaphoreType.REGULAR((n // 2,)),
            ],
            compiler_params=pltpu.CompilerParams(
                collective_id=0, has_side_effects=True, vmem_limit_bytes=44 * 1024 * 1024
            ),
        )(*(pltpu.with_memory_space_constraint(x, pltpu.HBM) for x in operands))

    placed = (P(("rep", "seq"), None),) * 3 + (P(),) * 5
    return jax.shard_map(
        body, mesh=mesh, in_specs=placed, out_specs=P(("rep", "seq"), None), check_vma=False
    )
```

time: 16.3 us -> 14.5 us (0.89)
  Pallas kernels: 15.3 us -> 13.5 us
    pallas_call x1, Pallas kernels: 15.3 us -> 13.5 us  [body(): pl.pallas_call(functools.partial(kernel, n, width), out_shape=pltpu.VMEM(...]
where the time goes in v2:
time: 14.5 us; the launch traced here: 14.3 us
  Pallas kernels  13.5 us (93%)
  local copies, waits for them, and re-layouts  0.8 us (6%)
    pallas_call x1, Pallas kernels, body(): pl.pallas_call(functools.partial(kernel, n, width), out_shape=pltpu.VMEM(...  13.5 us
    unnamed x1, local copies, waits for them, and re-layouts  0.8 us

profile of v2, /device:TPU:29, one launch (start us, length us, event | category | flops | bytes accessed | tf_op | source)
XLA Modules:
  0.0 14.3 jit_solution(17119010837154295580)
XLA Ops:
  0.0 13.5 %shard_map.82 = bf16[128,2048]{1,0:T(8,128)(2,1)S(1)} custom-call(bf16[128,2048]{1,0:T(8,128)(2,1)} %q_hbm.1, bf16[128,2048]{1,0:T(8,128)(2,1)} %k_hbm.1, bf16[128,2048]{1,0:T(8,128)(2,1)} %v_hbm.1, f32[3,3,2048]{2,1,0:T(4,128)} %taps_hbm.1, f32[16,2048]{1,0:T(8,128)} %bitcast.3, f32[16,2048]{1,0:T(8,128)} %bitcast.4, f32[1,2048]{1,0:T(1,128)} %bitcast.5, ...), custom_call_target="tpu_custom_call" | custom-call | tf_op jit(solution)/shard_map/pallas_call | solution.py:402
  13.5 0.8 %copy.10 = bf16[128,2048]{1,0:T(8,128)(2,1)} copy(bf16[128,2048]{1,0:T(8,128)(2,1)S(1)} %shard_map.82) | data formatting | bytes 1048576

commit v3 on v2

--- a/solution.py
+++ b/solution.py
@@ -20,9 +20,9 @@
     q_hbm, k_hbm, v_hbm, taps_hbm, rates_hbm, residue_hbm, skip_hbm, w_hbm,
     out_ref,
     q_in, k_in, v_in, taps_ref, rates_ref, residue_ref, skip_ref, w_in,
-    tails_out, tails_in, order, moved, fade_ref, skip2_ref, stride_ref, span_ref, weight_ref,
-    filter_ref, edge, sig, q_short, partial, local, segments, turn, natural,
-    gated, entry, ends, before, totals, earlier, total_out,
+    tails_out, tails_in, order, moved, fresh, fade_ref, skip2_ref, stride_ref, span_ref, weight_ref,
+    filter_ref, edge, sig, q_short, partial, local, segments, turn, work, natural,
+    gated, entry, ends, before, totals, earlier,
     in_sems, w_sem, tail_sems, pair_send, pair_recv, group_send, group_recv, credits,
 ):
     rows, chans = q_in.shape
@@ -34,6 +34,7 @@
     me = lax.axis_index("seq")
     group = lax.div(me, 2)
     odd = lax.rem(me, 2)
+    zero = lax.div(me, n)
 
     barrier = pltpu.get_barrier_semaphore()
 
@@ -96,8 +97,6 @@
     def _():
         before[...] = jnp.zeros_like(before)
 
-    total_out[...] = jnp.zeros_like(total_out)
-    natural[...] = jnp.zeros_like(natural)
     lane_row = lax.broadcasted_iota(jnp.int32, (SUB, LANES), 0)
     lane_step = lane_row.astype(F32)
 
@@ -144,14 +143,14 @@
         return x.astype(BF16).astype(F32)
 
     def mix(c, carry):
-        slot = lax.rem(c, 2)
         following = jnp.minimum(c + 1, strips - 1)
-        next_k = arrange(k_in, following)
-        next_v = arrange(v_in, following)
+        moved[:2] = fresh[...]
+        fresh[0] = arrange(k_in, following)
+        fresh[1] = arrange(v_in, following)
         for half in range(wide // LANES):
             cols = columns(c * (wide // LANES) + half)
-            xk = moved.at[slot, 0, :, half * LANES : (half + 1) * LANES]
-            xv = moved.at[slot, 1, :, half * LANES : (half + 1) * LANES]
+            xk = moved.at[0, :, half * LANES : (half + 1) * LANES]
+            xv = moved.at[1, :, half * LANES : (half + 1) * LANES]
             k_taps = tap_rows(1, cols)
             v_taps = tap_rows(2, cols)
             for i in range(2):
@@ -166,12 +165,12 @@
                     state[m] = u if i == 2 else state[m] * fades[m] + u
             for m in range(modes):
                 local[m * SUB : (m + 1) * SUB, cols] = state[m]
-        moved[1 - slot, 0] = next_k
-        moved[1 - slot, 1] = next_v
-        return carry
-
-    moved[0, 0] = arrange(k_in, 0)
-    moved[0, 1] = arrange(v_in, 0)
+            for m in range(0, modes, 4):
+                moved[zero + 2, m // 4 * SUB : (m // 4 + 1) * SUB, :LANES] = state[m + 3]
+        return carry
+
+    fresh[0] = arrange(k_in, 0)
+    fresh[1] = arrange(v_in, 0)
     first_cells = strips // 3
     lax.fori_loop(0, first_cells, mix, 0)
 
@@ -255,9 +254,27 @@
 
     lax.fori_loop(0, chunks, summaries, 0)
 
+    def combine(g):
+        pair_copy(g).wait_recv()
+
+        @pl.when(group < groups - 1)
+        def _():
+            totals[g] = (span_ref[:, chunk(g)] * before[g] + ends[g]).astype(totals.dtype)
+
+            def send(target, inner):
+                @pl.when(g == 0)
+                def _():
+                    pl.semaphore_wait(credits.at[target], 2)
+
+                for core in range(2):
+                    group_copy(group, target, core, g).start()
+                return inner
+
+            lax.fori_loop(group + 1, groups, send, 0)
+
     def direct(c, carry):
-        slot = lax.rem(c, 2)
-        next_q = arrange(q_in, jnp.minimum(c + 1, strips - 1))
+        moved[0] = fresh[0]
+        fresh[0] = arrange(q_in, jnp.minimum(c + 1, strips - 1))
         for half in range(wide // LANES):
             cols = columns(c * (wide // LANES) + half)
             response = [jnp.zeros((SUB, LANES), F32) for _ in range(steps // SUB)]
@@ -272,7 +289,7 @@
             response[0] = response[0] + jnp.where(lane_row == 0, skip_ref[:, cols], 0.0)
             for b in range(steps // SUB):
                 filter_ref[half, b * SUB : (b + 1) * SUB, :] = response[b]
-            xq = moved.at[slot, 0, :, half * LANES : (half + 1) * LANES]
+            xq = moved.at[0, :, half * LANES : (half + 1) * LANES]
             q_taps = tap_rows(0, cols)
             q0, q1 = ends_of(0, cols, short(xq, q_taps, 0), short(xq, q_taps, 1))
             taps = [filter_ref[half, i : i + 1, :] for i in range(steps)]
@@ -283,64 +300,43 @@
                 for s in range(i):
                     acc = acc + taps[i - s] * signal[s]
                 partial[i, :, cols] = acc
-        moved[1 - slot, 0] = next_q
-        return carry
-
-    moved[0, 0] = arrange(q_in, 0)
-    lax.fori_loop(0, strips, direct, 0)
-
-    @pl.when(odd == 1)
-    def _():
-        def combine(g, carry):
-            pair_copy(g).wait_recv()
-
-            @pl.when(group < groups - 1)
-            def _():
-                totals[g] = (span_ref[:, chunk(g)] * before[g] + ends[g]).astype(totals.dtype)
-
-                def send(target, inner):
-                    @pl.when(g == 0)
-                    def _():
-                        pl.semaphore_wait(credits.at[target], 2)
-
-                    for core in range(2):
-                        group_copy(group, target, core, g).start()
-                    return inner
-
-                lax.fori_loop(group + 1, groups, send, 0)
-
-            return carry
-
-        lax.fori_loop(0, chunks, combine, 0)
-
-    w_load.wait()
-    tile = out_ref.shape[1] // cells
-
-    def gather_gated():
-        for k in range(cells):
-            gated[:, k * LANES : (k + 1) * LANES] = natural[k].astype(BF16)
-
-    def project(g, k):
-        here = slice(k * tile, (k + 1) * tile)
-        return jnp.dot(gated[...], w_in[chunk(g), here], preferred_element_type=F32)
-
-    def output(g, k):
+        return carry
+
+    fresh[0] = arrange(q_in, 0)
+    lead = strips // 2
+    lax.fori_loop(0, lead, direct, 0)
+
+    def combine_and_direct(g, carry):
+        @pl.when(odd == 1)
+        def _():
+            combine(g)
+
+        return lax.fori_loop(lead + g * (strips - lead) // chunks, lead + (g + 1) * (strips - lead) // chunks, direct, carry)
+
+    lax.fori_loop(0, chunks, combine_and_direct, 0)
+
+    def enter(g, k):
         cols = columns(g * cells + k)
         state = entry[:, k * LANES : (k + 1) * LANES]
         stride = stride_ref[:, cols]
         for j in range(SUB):
-            turn[k, j * modes : (j + 1) * modes, :] = state
+            work[k, j * modes : (j + 1) * modes, :] = state
             if j + 1 < SUB:
                 state = state * stride + segments[j, :, cols]
-        flow = [turn[k, pl.ds(m, SUB, stride=modes), :] for m in range(modes)]
+
+    def output(g, k):
+        cols = columns(g * cells + k)
+        flow = [work[k, pl.ds(m, SUB, stride=modes), :] for m in range(modes)]
+        fades = [fade_ref[m : m + 1, cols] for m in range(modes)]
         for i in range(steps):
             terms = list(flow)
             while len(terms) > 1:
                 terms = [sum(terms[a : a + 2]) for a in range(0, len(terms), 2)]
             long_out = rounded(partial[i, :, cols] + terms[0])
-            natural[k, pl.ds(i, SUB, stride=steps), :] = q_short[i, :, cols] * long_out
+            natural[pl.ds(i, SUB, stride=steps), :] = q_short[i, :, cols] * long_out
             if i + 1 < steps:
-                flow = [flow[m] * fade_ref[m : m + 1, cols] for m in range(modes)]
+                flow = [flow[m] * fades[m] for m in range(modes)]
+        gated[g * cells + k] = natural[...].astype(BF16)
 
     def finish(g, carry):
         span = span_ref[:, chunk(g)]
@@ -352,17 +348,22 @@
 
         entering = lax.fori_loop(0, group, gather, jnp.zeros((modes, width), F32))
         entry[...] = jnp.where(odd == 1, span, 1.0) * entering + before[g]
-        gather_gated()
         for k in range(cells):
-            total_out[:, k * tile : (k + 1) * tile] += project(jnp.maximum(g - 1, 0), k)
+            enter(g, k)
+
+        def one(k, inner):
             output(g, k)
+            return inner
+
+        lax.fori_loop(0, cells, one, 0)
         return carry
 
     lax.fori_loop(0, chunks, finish, 0)
-    gather_gated()
-    for k in range(cells):
-        here = slice(k * tile, (k + 1) * tile)
-        out_ref[:, here] = (total_out[:, here] + project(chunks - 1, k)).astype(out_ref.dtype)
+    w_load.wait()
+    rows_in = jnp.concatenate([gated[c] for c in range(chans // LANES)], axis=1)
+    for a in range(0, out_ref.shape[1], 2 * LANES):
+        piece = jnp.dot(rows_in, w_in[:, a : a + 2 * LANES], preferred_element_type=F32)
+        out_ref[:, a : a + 2 * LANES] = piece.astype(out_ref.dtype)
 
     @pl.when(me < n - 1)
     def _():
@@ -413,7 +414,8 @@
                 pltpu.VMEM((SUB, chans), F32),
                 pltpu.VMEM((SUB, chans), F32),
                 pltpu.VMEM(((steps + 2) * SUB, rows), BF16),
-                pltpu.VMEM((2, 2, (steps + 2) * SUB, min(width, 2 * LANES)), F32),
+                pltpu.VMEM((3, (steps + 2) * SUB, min(width, 2 * LANES)), F32),
+                pltpu.VMEM((2, (steps + 2) * SUB, min(width, 2 * LANES)), F32),
                 table, table, table, table, table,
                 pltpu.VMEM((2, steps, LANES), F32),
                 pltpu.VMEM((4, SUB, chans), F32),
@@ -421,14 +423,14 @@
                 pltpu.VMEM((modes * SUB, chans), F32),
                 pltpu.VMEM((SUB, modes, chans), F32),
                 pltpu.VMEM((width // LANES, modes * SUB, LANES), F32),
-                pltpu.VMEM((width // LANES, rows, LANES), F32),
-                pltpu.VMEM((rows, width), BF16),
+                pltpu.VMEM((width // LANES, modes * SUB, LANES), F32),
+                pltpu.VMEM((rows, LANES), F32),
+                pltpu.VMEM((chans // LANES, rows, LANES), BF16),
                 pltpu.VMEM((modes, width), F32),
                 pltpu.VMEM((chunks, modes, width), F32),
                 pltpu.VMEM((chunks, modes, width), F32),
                 pltpu.VMEM((chunks, modes, width), BF16),
                 pltpu.VMEM((n // 2, chunks, modes, width), BF16),
-                pltpu.VMEM((rows, w_out.shape[1]), F32),
                 dma((7,)),
                 dma,
                 dma((2,)),

time: 14.5 us -> 12.9 us (0.89)
  the two profiles are of different devices: /device:TPU:29 before, /device:TPU:31 now
where the time goes in v3:
time: 12.9 us; the launch traced here: 12.8 us
  Pallas kernels  12 us (93%)
  local copies, waits for them, and re-layouts  0.8 us (6%)
    pallas_call x1, Pallas kernels, body(): pl.pallas_call(functools.partial(kernel, n, width), out_shape=pltpu.VMEM(...  12 us
    unnamed x1, local copies, waits for them, and re-layouts  0.8 us

profile of v3, /device:TPU:31, one launch (start us, length us, event | category | flops | bytes accessed | tf_op | source)
XLA Modules:
  0.0 12.8 jit_solution(18087940123286368138)
XLA Ops:
  0.0 12.0 %shard_map.82 = bf16[128,2048]{1,0:T(8,128)(2,1)S(1)} custom-call(bf16[128,2048]{1,0:T(8,128)(2,1)} %q_hbm.1, bf16[128,2048]{1,0:T(8,128)(2,1)} %k_hbm.1, bf16[128,2048]{1,0:T(8,128)(2,1)} %v_hbm.1, f32[3,3,2048]{2,1,0:T(4,128)} %taps_hbm.1, f32[16,2048]{1,0:T(8,128)} %bitcast.3, f32[16,2048]{1,0:T(8,128)} %bitcast.4, f32[1,2048]{1,0:T(1,128)} %bitcast.5, ...), custom_call_target="tpu_custom_call" | custom-call | tf_op jit(solution)/shard_map/pallas_call | solution.py:403
  12.0 0.8 %copy.10 = bf16[128,2048]{1,0:T(8,128)(2,1)} copy(bf16[128,2048]{1,0:T(8,128)(2,1)S(1)} %shard_map.82) | data formatting | bytes 1048576

commit v4 on v3

--- a/solution.py
+++ b/solution.py
@@ -20,10 +20,10 @@
     q_hbm, k_hbm, v_hbm, taps_hbm, rates_hbm, residue_hbm, skip_hbm, w_hbm,
     out_ref,
     q_in, k_in, v_in, taps_ref, rates_ref, residue_ref, skip_ref, w_in,
-    tails_out, tails_in, order, moved, fresh, fade_ref, skip2_ref, stride_ref, span_ref, weight_ref,
+    tails_out, tails_in, tails, order, moved, fresh, fade_ref, skip2_ref, stride_ref, span_ref, weight_ref,
     filter_ref, edge, sig, q_short, partial, local, segments, turn, work, natural,
-    gated, entry, ends, before, totals, earlier,
-    in_sems, w_sem, tail_sems, pair_send, pair_recv, group_send, group_recv, credits,
+    gated, entry, entries, shared, ends, other, totals, earlier,
+    in_sems, w_sem, tail_sems, pair_send, pair_recv, group_send, group_recv, share_send, share_recv, credits,
 ):
     rows, chans = q_in.shape
     modes = rates_ref.shape[0]
@@ -45,13 +45,11 @@
     def _():
         greet(me - 1)
 
-    @pl.when(odd == 1)
-    def _():
-        def later(device, carry):
-            greet(device)
-            return carry
-
-        lax.fori_loop(me + 1, n, later, 0)
+    def later(target, carry):
+        greet(2 * target + odd)
+        return carry
+
+    lax.fori_loop(group + 1, groups, later, 0)
 
     loads = [
         pltpu.make_async_copy(src, dst, in_sems.at[i])
@@ -63,7 +61,6 @@
     for load in loads:
         load.start()
     w_load = pltpu.make_async_copy(w_hbm, w_in, w_sem)
-    w_load.start()
 
     def tail_copy():
         return pltpu.make_async_remote_copy(
@@ -73,15 +70,24 @@
 
     def pair_copy(g):
         return pltpu.make_async_remote_copy(
-            src_ref=ends.at[g], dst_ref=before.at[g], send_sem=pair_send.at[g], recv_sem=pair_recv.at[g],
+            src_ref=ends.at[g], dst_ref=other.at[g], send_sem=pair_send.at[g], recv_sem=pair_recv.at[g],
             device_id={"seq": me + 1 - 2 * odd}, device_id_type=MESH,
         )
 
-    def group_copy(source, target, core, g):
+    def keeper(g):
+        return lax.div(2 * g, chunks)
+
+    def group_copy(source, target, g):
         return pltpu.make_async_remote_copy(
             src_ref=totals.at[g], dst_ref=earlier.at[source, g],
-            send_sem=group_send.at[target, core, g], recv_sem=group_recv.at[source, g],
-            device_id={"seq": 2 * target + core}, device_id_type=MESH,
+            send_sem=group_send.at[target, g], recv_sem=group_recv.at[source, g],
+            device_id={"seq": 2 * target + odd}, device_id_type=MESH,
+        )
+
+    def share_copy(g):
+        return pltpu.make_async_remote_copy(
+            src_ref=entries.at[g], dst_ref=shared.at[g], send_sem=share_send.at[g], recv_sem=share_recv.at[g],
+            device_id={"seq": me + 1 - 2 * odd}, device_id_type=MESH,
         )
 
     place = lax.broadcasted_iota(jnp.int32, order.shape, 0)
@@ -93,9 +99,16 @@
     def _():
         tails_in[...] = jnp.zeros_like(tails_in)
 
+    half = (chunks + 1) // 2
+
     @pl.when(odd == 0)
     def _():
-        before[...] = jnp.zeros_like(before)
+        for g in range(half, chunks):
+            other[g] = jnp.zeros(other.shape[1:], F32)
+
+    @pl.when(group == 0)
+    def _():
+        shared[...] = jnp.zeros_like(shared)
 
     lane_row = lax.broadcasted_iota(jnp.int32, (SUB, LANES), 0)
     lane_step = lane_row.astype(F32)
@@ -122,6 +135,25 @@
     for load in loads[1:4]:
         load.wait()
 
+    loads[5].wait()
+    w_load.start()
+    last = [tokens[rows - 16 :, :].astype(F32)[14:16] for tokens in (q_in, k_in, v_in)]
+    tails_out[...] = jnp.concatenate(last + [jnp.zeros((2, chans), F32)], axis=0).astype(BF16)
+
+    pl.semaphore_wait(barrier, jnp.where(me < n - 1, 1, 0) + group)
+
+    @pl.when(me < n - 1)
+    def _():
+        tail_copy().start()
+
+    def credit(source, carry):
+        pl.semaphore_signal(
+            credits.at[group], inc=1, device_id={"seq": 2 * source + odd}, device_id_type=MESH
+        )
+        return carry
+
+    lax.fori_loop(0, group, credit, 0)
+
     def short(x, taps, i):
         result = taps[0] * x[SUB * (i + 2) : SUB * (i + 3)]
         result = result + taps[1] * x[SUB * (i + 1) : SUB * (i + 2)]
@@ -143,7 +175,7 @@
         return x.astype(BF16).astype(F32)
 
     def mix(c, carry):
-        following = jnp.minimum(c + 1, strips - 1)
+        following = lax.rem(c + 1, strips)
         moved[:2] = fresh[...]
         fresh[0] = arrange(k_in, following)
         fresh[1] = arrange(v_in, following)
@@ -169,33 +201,9 @@
                 moved[zero + 2, m // 4 * SUB : (m // 4 + 1) * SUB, :LANES] = state[m + 3]
         return carry
 
-    fresh[0] = arrange(k_in, 0)
-    fresh[1] = arrange(v_in, 0)
-    first_cells = strips // 3
-    lax.fori_loop(0, first_cells, mix, 0)
-
-    loads[5].wait()
-    for i, tokens in enumerate((q_in, k_in, v_in)):
-        last = tokens[rows - 16 :, :].astype(F32)
-        tails_out[2 * i : 2 * i + 2, :] = last[14:16]
-    tails_out[6:8, :] = jnp.zeros((2, chans), F32)
-
-    pl.semaphore_wait(barrier, jnp.where(me < n - 1, 1, 0) + group)
-
-    @pl.when(me < n - 1)
-    def _():
-        tail_copy().start()
-
-    def credit(source, carry):
-        pl.semaphore_signal(
-            credits.at[group], inc=1, device_id={"seq": 2 * source + 1}, device_id_type=MESH
-        )
-        return carry
-
-    lax.fori_loop(0, group, credit, 0)
-
-    lax.fori_loop(first_cells, strips, mix, 0)
-
+    opening = (1 - odd) * half * (strips // chunks)
+    fresh[0] = arrange(k_in, opening)
+    fresh[1] = arrange(v_in, opening)
     loads[4].wait()
     loads[6].wait()
 
@@ -206,16 +214,12 @@
 
     lax.fori_loop(0, chunks, residue_tables, 0)
 
-    @pl.when(me > 0)
-    def _():
-        tail_copy().wait_recv()
-
     head = lane_row == 0
 
     def ends_of(which, cols, zeroth, first):
         taps = tap_rows(which, cols)
         one, two = (
-            jnp.where(head, tails_in[2 * which + a : 2 * which + a + 1, cols], 0.0) for a in (1, 0)
+            jnp.where(head, tails[2 * which + a : 2 * which + a + 1, cols], 0.0) for a in (1, 0)
         )
         return zeroth + taps[1] * one + taps[2] * two, first + taps[2] * one
 
@@ -242,35 +246,63 @@
             state = part if j == 0 else state * stride + part
         ends[g, :, columns(c - g * cells)] = state
 
-    def summaries(g, carry):
-        for c in range(cells):
-            summarize(g * cells + c, g, c)
-
-        @pl.when(odd == 0)
-        def _():
-            pair_copy(g).start()
-
-        return carry
-
-    lax.fori_loop(0, chunks, summaries, 0)
-
     def combine(g):
         pair_copy(g).wait_recv()
 
         @pl.when(group < groups - 1)
         def _():
-            totals[g] = (span_ref[:, chunk(g)] * before[g] + ends[g]).astype(totals.dtype)
+            mine, theirs = ends[g], other[g]
+            former = jnp.where(odd == 1, theirs, mine)
+            latter = jnp.where(odd == 1, mine, theirs)
+            totals[g] = (span_ref[:, chunk(g)] * former + latter).astype(totals.dtype)
 
             def send(target, inner):
-                @pl.when(g == 0)
+                @pl.when(lax.rem(g, half) == 0)
                 def _():
-                    pl.semaphore_wait(credits.at[target], 2)
-
-                for core in range(2):
-                    group_copy(group, target, core, g).start()
+                    pl.semaphore_wait(credits.at[target], 1)
+
+                group_copy(group, target, g).start()
                 return inner
 
             lax.fori_loop(group + 1, groups, send, 0)
+
+    early = jnp.logical_or(me == 0, odd == 1)
+    share = strips // chunks
+
+    def stage(t, carry):
+        mixing = jnp.where(early, lax.rem(t, 2) == 0, t < chunks)
+        turn_at = jnp.where(early, lax.div(t, 2), lax.rem(t, chunks))
+        g = lax.rem(turn_at + (1 - odd) * half, chunks)
+        own = keeper(g) == odd
+
+        @pl.when(mixing)
+        def _():
+            lax.fori_loop(g * share, (g + 1) * share, mix, 0)
+
+        @pl.when(jnp.logical_not(mixing))
+        def _():
+            @pl.when(turn_at == 0)
+            def _():
+                @pl.when(me > 0)
+                def _():
+                    tail_copy().wait_recv()
+
+                tails[...] = tails_in[...].astype(F32)
+
+            for c in range(cells):
+                summarize(g * cells + c, g, c)
+
+            @pl.when(jnp.logical_or(odd == 0, jnp.logical_not(own)))
+            def _():
+                pair_copy(g).start()
+
+            @pl.when(jnp.logical_and(own, jnp.logical_or(odd == 0, me == 1)))
+            def _():
+                combine(g)
+
+        return carry
+
+    lax.fori_loop(0, 2 * chunks, stage, 0)
 
     def direct(c, carry):
         moved[0] = fresh[0]
@@ -303,17 +335,19 @@
         return carry
 
     fresh[0] = arrange(q_in, 0)
-    lead = strips // 2
+    lead = strips // 4
     lax.fori_loop(0, lead, direct, 0)
 
     def combine_and_direct(g, carry):
-        @pl.when(odd == 1)
+        @pl.when(jnp.logical_and(odd == 1, me > 1))
         def _():
             combine(g)
 
-        return lax.fori_loop(lead + g * (strips - lead) // chunks, lead + (g + 1) * (strips - lead) // chunks, direct, carry)
-
-    lax.fori_loop(0, chunks, combine_and_direct, 0)
+        done = lead + (g - half) * (strips - lead) // (chunks - half)
+        upto = lead + (g + 1 - half) * (strips - lead) // (chunks - half)
+        return lax.fori_loop(done, upto, direct, carry)
+
+    lax.fori_loop(half, chunks, combine_and_direct, 0)
 
     def enter(g, k):
         cols = columns(g * cells + k)
@@ -333,21 +367,44 @@
             while len(terms) > 1:
                 terms = [sum(terms[a : a + 2]) for a in range(0, len(terms), 2)]
             long_out = rounded(partial[i, :, cols] + terms[0])
-            natural[pl.ds(i, SUB, stride=steps), :] = q_short[i, :, cols] * long_out
+            natural[g * cells + k, pl.ds(i, SUB, stride=steps), :] = q_short[i, :, cols] * long_out
             if i + 1 < steps:
                 flow = [flow[m] * fades[m] for m in range(modes)]
-        gated[g * cells + k] = natural[...].astype(BF16)
-
-    def finish(g, carry):
+
+    def finish(s, carry):
+        g = lax.rem(s + odd * half, chunks)
+        own = keeper(g) == odd
         span = span_ref[:, chunk(g)]
         far = span * span
-
-        def gather(source, state):
-            group_copy(source, group, odd, g).wait_recv()
-            return state * far + earlier[source, g].astype(F32)
-
-        entering = lax.fori_loop(0, group, gather, jnp.zeros((modes, width), F32))
-        entry[...] = jnp.where(odd == 1, span, 1.0) * entering + before[g]
+        reach = jnp.where(odd == 1, span, 1.0)
+
+        @pl.when(own)
+        def _():
+            def gather(source, state):
+                group_copy(source, group, g).wait_recv()
+                return state * far + earlier[source, g].astype(F32)
+
+            entering = lax.fori_loop(0, group, gather, jnp.zeros((modes, width), F32))
+            entries[g] = entering
+
+            @pl.when(group > 0)
+            def _():
+                share_copy(g).start()
+
+            entry[...] = reach * entering + jnp.where(odd == 1, other[g], 0.0)
+
+        @pl.when(jnp.logical_not(own))
+        def _():
+            @pl.when(group > 0)
+            def _():
+                share_copy(g).wait_recv()
+
+            @pl.when(odd == 1)
+            def _():
+                pair_copy(g).wait_recv()
+
+            entry[...] = reach * shared[g] + jnp.where(odd == 1, other[g], 0.0)
+
         for k in range(cells):
             enter(g, k)
 
@@ -360,7 +417,9 @@
 
     lax.fori_loop(0, chunks, finish, 0)
     w_load.wait()
-    rows_in = jnp.concatenate([gated[c] for c in range(chans // LANES)], axis=1)
+    for c in range(chans // LANES):
+        gated[:, c * LANES : (c + 1) * LANES] = natural[c].astype(BF16)
+    rows_in = gated[...]
     for a in range(0, out_ref.shape[1], 2 * LANES):
         piece = jnp.dot(rows_in, w_in[:, a : a + 2 * LANES], preferred_element_type=F32)
         out_ref[:, a : a + 2 * LANES] = piece.astype(out_ref.dtype)
@@ -369,20 +428,27 @@
     def _():
         tail_copy().wait_send()
 
-    @pl.when(odd == 0)
+    for g in range(chunks):
+        kept = 2 * g // chunks
+
+        @pl.when(jnp.logical_or(odd == 0, odd != kept))
+        def _():
+            pair_copy(g).wait_send()
+
+        @pl.when(odd == kept)
+        def _():
+            def sent(target, carry):
+                group_copy(group, target, g).wait_send()
+                return carry
+
+            lax.fori_loop(group + 1, groups, sent, 0)
+
+    @pl.when(group > 0)
     def _():
         for g in range(chunks):
-            pair_copy(g).wait_send()
-
-    @pl.when(odd == 1)
-    def _():
-        def sent(target, carry):
-            for core in range(2):
-                for g in range(chunks):
-                    group_copy(group, target, core, g).wait_send()
-            return carry
-
-        lax.fori_loop(group + 1, groups, sent, 0)
+            @pl.when(odd == 2 * g // chunks)
+            def _():
+                share_copy(g).wait_send()
 
 
 def solution(mesh):
@@ -411,7 +477,8 @@
                 table, table,
                 pltpu.VMEM((1, chans), F32),
                 pltpu.VMEM(w_out.shape, BF16),
-                pltpu.VMEM((SUB, chans), F32),
+                pltpu.VMEM((SUB, chans), BF16),
+                pltpu.VMEM((SUB, chans), BF16),
                 pltpu.VMEM((SUB, chans), F32),
                 pltpu.VMEM(((steps + 2) * SUB, rows), BF16),
                 pltpu.VMEM((3, (steps + 2) * SUB, min(width, 2 * LANES)), F32),
@@ -424,9 +491,11 @@
                 pltpu.VMEM((SUB, modes, chans), F32),
                 pltpu.VMEM((width // LANES, modes * SUB, LANES), F32),
                 pltpu.VMEM((width // LANES, modes * SUB, LANES), F32),
-                pltpu.VMEM((rows, LANES), F32),
-                pltpu.VMEM((chans // LANES, rows, LANES), BF16),
+                pltpu.VMEM((chans // LANES, rows, LANES), F32),
+                tokens,
                 pltpu.VMEM((modes, width), F32),
+                pltpu.VMEM((chunks, modes, width), F32),
+                pltpu.VMEM((chunks, modes, width), F32),
                 pltpu.VMEM((chunks, modes, width), F32),
                 pltpu.VMEM((chunks, modes, width), F32),
                 pltpu.VMEM((chunks, modes, width), BF16),
@@ -436,8 +505,10 @@
                 dma((2,)),
                 dma((chunks,)),
                 dma((chunks,)),
-                dma((n // 2, 2, chunks)),
                 dma((n // 2, chunks)),
+                dma((n // 2, chunks)),
+                dma((chunks,)),
+                dma((chunks,)),
                 pltpu.SemaphoreType.REGULAR((n // 2,)),
             ],
             compiler_params=pltpu.CompilerParams(

time: 12.9 us -> 12.8 us (level)
  the two profiles are of different devices: /device:TPU:31 before, /device:TPU:29 now
where the time goes in v4:
time: 12.8 us; the launch traced here: 12.6 us
  Pallas kernels  11.8 us (92%)
  local copies, waits for them, and re-layouts  0.8 us (6%)
    pallas_call x1, Pallas kernels, body(): pl.pallas_call(functools.partial(kernel, n, width), out_shape=pltpu.VMEM(...  11.8 us
    unnamed x1, local copies, waits for them, and re-layouts  0.8 us

profile of v4, /device:TPU:29, one launch (start us, length us, event | category | flops | bytes accessed | tf_op | source)
XLA Modules:
  0.0 12.6 jit_solution(16836626255034547093)
XLA Ops:
  0.0 11.8 %shard_map.82 = bf16[128,2048]{1,0:T(8,128)(2,1)S(1)} custom-call(bf16[128,2048]{1,0:T(8,128)(2,1)} %q_hbm.1, bf16[128,2048]{1,0:T(8,128)(2,1)} %k_hbm.1, bf16[128,2048]{1,0:T(8,128)(2,1)} %v_hbm.1, f32[3,3,2048]{2,1,0:T(4,128)} %taps_hbm.1, f32[16,2048]{1,0:T(8,128)} %bitcast.3, f32[16,2048]{1,0:T(8,128)} %bitcast.4, f32[1,2048]{1,0:T(1,128)} %bitcast.5, ...), custom_call_target="tpu_custom_call" | custom-call | tf_op jit(solution)/shard_map/pallas_call | solution.py:469
  11.9 0.8 %copy.10 = bf16[128,2048]{1,0:T(8,128)(2,1)} copy(bf16[128,2048]{1,0:T(8,128)(2,1)S(1)} %shard_map.82) | data formatting | bytes 1048576

commit v5 on v4

--- a/solution.py
+++ b/solution.py
@@ -119,6 +119,16 @@
     def chunk(g):
         return pl.ds(pl.multiple_of(g * width, width), width)
 
+    pl.semaphore_wait(barrier, jnp.where(me < n - 1, 1, 0) + group)
+
+    def credit(source, carry):
+        pl.semaphore_signal(
+            credits.at[group], inc=1, device_id={"seq": 2 * source + odd}, device_id_type=MESH
+        )
+        return carry
+
+    lax.fori_loop(0, group, credit, 0)
+
     loads[0].wait()
 
     def rates_tables(g, carry):
@@ -140,19 +150,9 @@
     last = [tokens[rows - 16 :, :].astype(F32)[14:16] for tokens in (q_in, k_in, v_in)]
     tails_out[...] = jnp.concatenate(last + [jnp.zeros((2, chans), F32)], axis=0).astype(BF16)
 
-    pl.semaphore_wait(barrier, jnp.where(me < n - 1, 1, 0) + group)
-
     @pl.when(me < n - 1)
     def _():
         tail_copy().start()
-
-    def credit(source, carry):
-        pl.semaphore_signal(
-            credits.at[group], inc=1, device_id={"seq": 2 * source + odd}, device_id_type=MESH
-        )
-        return carry
-
-    lax.fori_loop(0, group, credit, 0)
 
     def short(x, taps, i):
         result = taps[0] * x[SUB * (i + 2) : SUB * (i + 3)]
@@ -335,19 +335,19 @@
         return carry
 
     fresh[0] = arrange(q_in, 0)
-    lead = strips // 4
+    lead = strips // 4 * jnp.minimum(group, 2)
+    lead = jnp.where(jnp.logical_and(odd == 1, me > 1), lead, strips)
     lax.fori_loop(0, lead, direct, 0)
 
-    def combine_and_direct(g, carry):
-        @pl.when(jnp.logical_and(odd == 1, me > 1))
-        def _():
+    @pl.when(jnp.logical_and(odd == 1, me > 1))
+    def _():
+        def each(g, carry):
             combine(g)
-
-        done = lead + (g - half) * (strips - lead) // (chunks - half)
-        upto = lead + (g + 1 - half) * (strips - lead) // (chunks - half)
-        return lax.fori_loop(done, upto, direct, carry)
-
-    lax.fori_loop(half, chunks, combine_and_direct, 0)
+            return carry
+
+        lax.fori_loop(half, chunks, each, 0)
+
+    lax.fori_loop(lead, strips, direct, 0)
 
     def enter(g, k):
         cols = columns(g * cells + k)
@@ -371,27 +371,29 @@
             if i + 1 < steps:
                 flow = [flow[m] * fades[m] for m in range(modes)]
 
+    def receive(s, carry):
+        g = s + odd * half
+        far = span_ref[:, chunk(g)]
+        far = far * far
+
+        def gather(source, state):
+            group_copy(source, group, g).wait_recv()
+            return state * far + earlier[source, g].astype(F32)
+
+        entries[g] = lax.fori_loop(0, group, gather, jnp.zeros((modes, width), F32))
+
+        @pl.when(group > 0)
+        def _():
+            share_copy(g).start()
+
+        return carry
+
+    lax.fori_loop(0, jnp.where(odd == 1, chunks - half, half), receive, 0)
+
     def finish(s, carry):
         g = lax.rem(s + odd * half, chunks)
         own = keeper(g) == odd
-        span = span_ref[:, chunk(g)]
-        far = span * span
-        reach = jnp.where(odd == 1, span, 1.0)
-
-        @pl.when(own)
-        def _():
-            def gather(source, state):
-                group_copy(source, group, g).wait_recv()
-                return state * far + earlier[source, g].astype(F32)
-
-            entering = lax.fori_loop(0, group, gather, jnp.zeros((modes, width), F32))
-            entries[g] = entering
-
-            @pl.when(group > 0)
-            def _():
-                share_copy(g).start()
-
-            entry[...] = reach * entering + jnp.where(odd == 1, other[g], 0.0)
+        reach = jnp.where(odd == 1, span_ref[:, chunk(g)], 1.0)
 
         @pl.when(jnp.logical_not(own))
         def _():
@@ -403,8 +405,8 @@
             def _():
                 pair_copy(g).wait_recv()
 
-            entry[...] = reach * shared[g] + jnp.where(odd == 1, other[g], 0.0)
-
+        entering = jnp.where(own, entries[g], shared[g])
+        entry[...] = reach * entering + jnp.where(odd == 1, other[g], 0.0)
         for k in range(cells):
             enter(g, k)
 

time: 12.8 us -> 12.7 us (level)
  no operation moved by 1% of the time
where the time goes in v5:
time: 12.7 us; the launch traced here: 12.5 us
  Pallas kernels  11.7 us (92%)
  local copies, waits for them, and re-layouts  0.8 us (6%)
    pallas_call x1, Pallas kernels, body(): pl.pallas_call(functools.partial(kernel, n, width), out_shape=pltpu.VMEM(...  11.7 us
    unnamed x1, local copies, waits for them, and re-layouts  0.8 us

profile of v5, /device:TPU:29, one launch (start us, length us, event | category | flops | bytes accessed | tf_op | source)
XLA Modules:
  0.0 12.5 jit_solution(10111694223709748187)
XLA Ops:
  0.0 11.7 %shard_map.82 = bf16[128,2048]{1,0:T(8,128)(2,1)S(1)} custom-call(bf16[128,2048]{1,0:T(8,128)(2,1)} %q_hbm.1, bf16[128,2048]{1,0:T(8,128)(2,1)} %k_hbm.1, bf16[128,2048]{1,0:T(8,128)(2,1)} %v_hbm.1, f32[3,3,2048]{2,1,0:T(4,128)} %taps_hbm.1, f32[16,2048]{1,0:T(8,128)} %bitcast.3, f32[16,2048]{1,0:T(8,128)} %bitcast.4, f32[1,2048]{1,0:T(1,128)} %bitcast.5, ...), custom_call_target="tpu_custom_call" | custom-call | tf_op jit(solution)/shard_map/pallas_call | solution.py:471
  11.7 0.8 %copy.10 = bf16[128,2048]{1,0:T(8,128)(2,1)} copy(bf16[128,2048]{1,0:T(8,128)(2,1)S(1)} %shard_map.82) | data formatting | bytes 1048576
